TPU v7x, 512 devices: a whole 4x8x8 slice. The times are simulated.
512 devices in a mesh: rows: 32 (over y_hi, z), feat: 16 (over y_lo, x, core).
Axes of the slice: x: 4, y: 8 (y_hi: 4, y_lo: 2; y = y_hi * 2 + y_lo), z: 8, core: 2. Of those that a mesh axis runs over, the one named last changes fastest.
Arguments:
- acts: bfloat16 [32768, 8192], P('rows', 'feat'), may hold values from -6 to 6
- out_grads: bfloat16 [32768, 8192], P('rows', 'feat'), may hold values from -6 to 6
- proj_in: bfloat16 [8192, 256], P('feat'), may hold values from -0.0625 to 0.0625
- proj_out: bfloat16 [8192, 256], P('feat'), may hold values from -0.0625 to 0.0625
- assignment: int32 [32768], P('rows'), may hold values from 0 to 255
- codes: int32 [4096, 65536], P('rows', 'feat'), may hold values from -128 to 127
- zero_points: int32 [65536], P('feat'), may hold values from -64 to 63
- scales: float32 [65536], P('feat'), may hold values from 2e-06 to 2e-05
Outputs:
- scores: float32 [256, 4096], P('feat', 'rows')
All inputs are finite; a program needn't handle non-finite values.
Results may differ from a plain program's by a relative error of at most 0.005.
Values may be sent and summed in bfloat16 or wider, within the bound.
No kernel may reach another device: no remote copies, remote signals or barrier semaphores. Data moves between devices by JAX's collectives and lax.ppermute only.
A program may use at most 64 MiB of HBM per device.

v0:
```python
import jax
import jax.numpy as jnp
from jax import lax
from jax.sharding import Mesh
from jax.sharding import PartitionSpec as P

RANK = 256
QUERIES = 256
ROWS = ("rows_0", "rows_1")


def own_block(blocks, axes, order):
    shape = [lax.axis_size(a) for a in axes]
    blocks = blocks.reshape(*shape, *blocks.shape[1:])
    blocks = blocks.transpose(*order, *range(len(axes), blocks.ndim))
    blocks = blocks.reshape(-1, *blocks.shape[len(axes) :])
    for k in order:
        blocks = lax.psum_scatter(blocks, axes[k], scatter_dimension=0, tiled=True)
    return blocks[0]


def cut_along(x, dim, size):
    before, after = (x.shape[:dim], x.shape[dim + 1 :])
    return jnp.moveaxis(x.reshape(*before, size, -1, *after), dim, 0)


def summed_rows(x, axes, order, dim):
    size = lax.axis_size(axes)
    return own_block(cut_along(x, dim, size), axes, order)


def summed_on_arrival(x, axis, dim):
    size = lax.axis_size(axis)
    blocks = lax.all_to_all(cut_along(x, dim, size), axis, 0, 0, tiled=True)
    return jnp.sum(blocks, axis=0)


def local(acts, out_grads, proj_in, proj_out, assignment, codes, zero_points, scales):
    feat_count = lax.axis_size("feat")
    local_rank = RANK // feat_count
    tokens_here = acts.shape[0]
    part_inner = jnp.dot(acts, proj_in, preferred_element_type=jnp.float32)
    part_outer = jnp.dot(out_grads, proj_out, preferred_element_type=jnp.float32)
    summed_inner, summed_outer = lax.psum((part_inner, part_outer), "feat")
    outer_local = lax.dynamic_slice_in_dim(
        summed_outer, lax.axis_index("feat") * local_rank, local_rank, 1
    )
    inner16 = summed_inner.astype(jnp.bfloat16)
    outer16 = outer_local.astype(jnp.bfloat16)
    query_ids = lax.broadcasted_iota(jnp.int32, (1, QUERIES), 1)
    onehot = (assignment[:, None] == query_ids).astype(jnp.bfloat16)
    weighted = (onehot[:, :, None] * outer16[:, None, :]).reshape(tokens_here, QUERIES * local_rank)
    partial_grads = lax.dot_general(
        weighted, inner16, (((0,), (0,)), ((), ())), preferred_element_type=jnp.float32
    )
    partial_grads = partial_grads.reshape(QUERIES, local_rank * RANK)
    store16 = (codes - zero_points[None, :]).astype(jnp.bfloat16)
    share = summed_rows(partial_grads, ROWS, (1, 0), 0)
    share16 = (share * scales[None, :]).astype(jnp.bfloat16)
    terms = lax.dot_general(
        lax.all_gather(share16, ROWS, axis=0, tiled=True),
        store16,
        (((1,), (1,)), ((), ())),
        preferred_element_type=jnp.float32,
    )
    scores = summed_on_arrival(terms, "feat", 0)
    return scores


def solution(mesh):
    split = Mesh(mesh.devices.reshape(4, 8, mesh.shape["feat"]), ("rows_0", "rows_1", "feat"))
    in_specs = (
        P(ROWS, "feat"),
        P(ROWS, "feat"),
        P("feat", None),
        P("feat", None),
        P(ROWS),
        P(ROWS, "feat"),
        P("feat"),
        P("feat"),
    )
    out_specs = P("feat", ROWS)
    return jax.shard_map(local, mesh=split, in_specs=in_specs, out_specs=out_specs, check_vma=False)
```

profile of v0, /device:TPU:1, one launch (start us, length us, event | category | flops | bytes accessed | tf_op | source)
XLA Modules:
  0.0 298.8 jit_solution(7111749485750462943)
XLA Ops:
  6.5 0.0 copy-start
  6.5 0.0 reduce-scatter.3.cloned.1.call-start
  6.5 1.7 fusion.2
  8.2 0.0 copy-done
  8.2 1.4 fusion.7
  9.6 1.7 fusion.6
  11.4 68.3 %all-reduce.2 = (bf16[1024,256]{0,1:T(8,128)(2,1)}, bf16[1024,256]{1,0:T(8,128)(2,1)}) all-reduce(f32[1024,256]{0,1:T(8,128)S(1)} %fusion.6, f32[1024,256]{1,0:T(8,128)S(1)} %fusion.7), channel_id=1, replica_groups=mesh['rows_0'=4,'rows_1'=8,'feat'=16] {'feat'}, use_global_device_ids=true, to_apply=%region_0.0 | all-reduce | flops 524288 | bytes 3145728 | tf_op jit(solution)/shard_map/psum | solution.py:44
  79.6 0.8 dynamic-slice_convert_fusion
  80.4 0.0 copy-start.4
  80.4 1.8 broadcast_multiply_fusion
  82.2 0.0 copy-done.4
  82.2 4.3 %fusion.8 = f32[4096,256]{1,0:T(8,128)} fusion(bf16[1024,4096]{0,1:T(8,128)(2,1)S(1)} %bitcast.17, bf16[1024,256]{1,0:T(8,128)(2,1)S(1)} %copy-done.4), kind=kOutput, calls=%fused_computation.13 | convolution fusion | flops 2147483648 | bytes 13107200 | tf_op jit(solution)/shard_map/dot_general | solution.py:53
  86.5 4.9 %reshape_reshape_reshape.3 = f32[4,8,8,4096]{3,2,1,0:T(8,128)} reshape(f32[4096,256]{1,0:T(8,128)} %fusion.8) | data formatting | bytes 8388608 | tf_op jit(solution)/shard_map/reshape;reshape;reshape | solution.py:14
  91.4 4.6 %copy.10 = f32[4,8,8,4096]{3,2,0,1:T(8,128)} copy(f32[4,8,8,4096]{3,2,1,0:T(8,128)} %reshape_reshape_reshape.3) | data formatting | bytes 8388608 | tf_op jit(solution)/shard_map/reshape;reshape;reshape | solution.py:14
  96.1 0.0 copy-start.3
  96.1 0.0 copy-start.1
  96.1 0.0 copy-start.2
  96.1 0.0 reduce-scatter.3.cloned.1.call-update
  96.1 0.0 reduce-scatter.5.cloned.1.call-start
  96.1 62.0 %reduce-scatter.3.cloned.1.call-done = f32[4,8,4096]{2,1,0:T(8,128)} async-done(((f32[32,8,4096]{2,1,0:T(8,128)}), f32[4,8,4096]{2,1,0:T(8,128)}) %reduce-scatter.3.cloned.1.call-update) | async-done | bytes 524304 | tf_op jit(solution)/shard_map/reduce_scatter | solution.py:18
  158.2 0.0 reduce-scatter.5.cloned.1.call-update
  158.2 0.0 all-gather.2.cloned.1.call-start
  158.3 29.3 %reduce-scatter.5.cloned.1.call-done = f32[1,8,4096]{2,1,0:T(8,128)} async-done(((f32[4,8,4096]{2,1,0:T(8,128)}), f32[1,8,4096]{2,1,0:T(8,128)}) %reduce-scatter.5.cloned.1.call-update) | async-done | bytes 131088 | tf_op jit(solution)/shard_map/reduce_scatter | solution.py:18
  187.5 0.0 copy-done.3
  187.5 1.5 fusion.5
  189.0 0.0 all-gather.2.cloned.1.call-update
  189.1 85.2 %all-gather.2.cloned.1.call-done = bf16[256,4096]{1,0:T(8,128)(2,1)} async-done(((bf16[8,4096]{1,0:T(8,128)(2,1)}), bf16[256,4096]{1,0:T(8,128)(2,1)}) %all-gather.2.cloned.1.call-update) | async-done | bytes 2097168 | tf_op jit(solution)/shard_map/all_gather | solution.py:61
  274.3 0.0 copy-done.1
  274.3 0.0 copy-done.2
  274.3 2.3 fusion
  276.6 15.1 %all_to_all.5 = f32[16,16,128]{2,1,0:T(8,128)S(1)} all-to-all(f32[16,16,128]{2,1,0:T(8,128)S(1)} %bitcast.18), channel_id=1, replica_groups=mesh['rows_0'=4,'rows_1'=8,'feat'=16] {'feat'}, dimensions={0} | all-to-all | bytes 262144 | tf_op jit(solution)/shard_map/all_to_all | solution.py:34
  291.7 0.6 reduce_sum.9
Async XLA Ops:
  6.5 1.7 copy-start
  6.5 151.6 %reduce-scatter.3.cloned.1.call-start = ((), (), s32[]{:S(2)}) async-start(), calls=%async_computation.3 | async-start | bytes 4718592 | tf_op jit(solution)/shard_map/reduce_scatter | solution.py:18
  80.4 1.8 copy-start.4
  96.1 91.5 %copy-start.3 = (f32[4096]{0:T(1024)S(1)}, f32[4096]{0:T(1024)}, u32[]{:S(2)}) copy-start(f32[4096]{0:T(1024)} %param.15) | copy-start | bytes 49156
  96.1 178.2 %copy-start.1 = (s32[128,4096]{1,0:T(8,128)S(1)}, s32[128,4096]{1,0:T(8,128)}, u32[]{:S(2)}) copy-start(s32[128,4096]{1,0:T(8,128)} %param.13) | copy-start | bytes 6291460
  96.1 178.2 %copy-start.2 = (s32[4096]{0:T(1024)S(1)}, s32[4096]{0:T(1024)}, u32[]{:S(2)}) copy-start(s32[4096]{0:T(1024)} %param.14) | copy-start | bytes 49156
  96.1 91.4 %reduce-scatter.5.cloned.1.call-start = ((), (), s32[]{:S(2)}) async-start(), calls=%async_computation.4 | async-start | bytes 655360 | tf_op jit(solution)/shard_map/reduce_scatter | solution.py:18
  158.2 116.1 %all-gather.2.cloned.1.call-start = ((), (), s32[]{:S(2)}) async-start(), calls=%async_computation.5 | async-start | bytes 2162688 | tf_op jit(solution)/shard_map/all_gather | solution.py:61
Sparse Core Ops, SparseCore 0:
  96.2 61.9 reduce-scatter.2
  161.0 26.4 reduce-scatter.4
  190.7 83.5 all-gather.1
where the time goes:
time: 299 us
  waiting for transfers between devices  177 us (59%)
  blocking collectives  83.4 us (28%)
  between operations  13.1 us (4%)
  local copies, waits for them, and re-layouts  10.3 us (3%)
  matrix products  9.74 us (3%)
  other arithmetic  5.6 us (2%)
    reduce_scatter x2, waiting for transfers between devices, own_block(): blocks = lax.psum_scatter(blocks, axes[k], scatter_dimension=0, tiled=True)  91.3 us
    all_gather x1, waiting for transfers between devices, local(): lax.all_gather(share16, ROWS, axis=0, tiled=True)  85.2 us
    psum x1, blocking collectives, local(): summed_inner, summed_outer = lax.psum((part_inner, part_outer), 'feat')  68.3 us
    all_to_all x1, blocking collectives, summed_on_arrival(): blocks = lax.all_to_all(cut_along(x, dim, size), axis, 0, 0, tiled=True)  15.1 us
    another operation x2, local copies, waits for them, and re-layouts, own_block(): blocks = blocks.reshape(*shape, *blocks.shape[1:])  9.55 us
  transfers between devices with their start and end apart: 3, of which 3 were waited for; matrix products, arithmetic and copies ran while one was open for 0% of the time, Pallas kernels for 0%

commit v1 on v0

v1 whole, which is shorter than its diff:
```python
import jax
import jax.numpy as jnp
from jax import lax
from jax.experimental import pallas as pl
from jax.experimental.pallas import tpu as pltpu
from jax.sharding import Mesh
from jax.sharding import PartitionSpec as P

RANK = 256
QUERIES = 256
AXES = ("yh", "z", "yl", "x", "c")
ROWS = ("yh", "z")
FEAT = ("yl", "x", "c")
NZ = 8
NW = 8
NF = 16
NI = 16
NJ = 32
LINK_GAIN = 256.0
f32 = jnp.float32
bf16 = jnp.bfloat16
f16 = jnp.float16


def exchange(blocks, axes):
    return lax.all_to_all(blocks, axes, 0, 0, tiled=True)


def spread(block, axes, size):
    return exchange(jnp.broadcast_to(block[None], (size, *block.shape)), axes)


def store_kernel(codes_ref, zero_ref, out_ref):
    for i in range(codes_ref.shape[1] // RANK):
        cols = slice(i * RANK, (i + 1) * RANK)
        levels = (codes_ref[:, cols] - zero_ref[:, cols]).astype(f32)
        out_ref[:, i, :, :] = levels.T.astype(bf16).reshape(NZ, NJ, levels.shape[0])


def store_levels(codes, zero_points):
    rows = codes.shape[0]
    step = 4
    return pl.pallas_call(
        store_kernel,
        grid=(NI // step,),
        in_specs=[
            pl.BlockSpec((rows, step * RANK), lambda g: (0, g)),
            pl.BlockSpec((1, step * RANK), lambda g: (0, g)),
        ],
        out_specs=pl.BlockSpec((NZ, step, NJ, rows), lambda g: (0, g, 0, 0)),
        out_shape=jax.ShapeDtypeStruct((NZ, NI, NJ, rows), bf16),
        name="store_levels",
    )(codes, zero_points.reshape(1, -1))


def grads_kernel(inner_ref, outer_ref, scale_ref, out_ref, acc):
    acc[...] = jnp.zeros_like(acc)
    half = inner_ref.shape[2]
    query = lax.broadcasted_iota(jnp.int32, (QUERIES, half), 0).astype(f32)

    def row(r, carry):
        owners = outer_ref[r, 2 * NI : 2 * NI + 8, :].astype(f32)
        for h in range(2):
            outer = outer_ref[r, h * NI : (h + 1) * NI, :].astype(f32)
            inner = inner_ref[2 * r + h].astype(f32)
            product = (outer[:, None, :] * inner[None, :, :]).reshape(NI * NJ, half)
            high = product.astype(bf16)
            low = (product - high.astype(f32)).astype(bf16)
            mine = jnp.where(query == owners[h : h + 1, :], 1.0, 0.0).astype(bf16)
            dims = (((1,), (1,)), ((), ()))
            acc[...] += lax.dot_general(high, mine, dims, preferred_element_type=f32) + lax.dot_general(
                low, mine, dims, preferred_element_type=f32
            )
        return carry

    lax.fori_loop(0, NZ, row, 0)
    out_ref[...] = (acc[...].T * scale_ref[...]).astype(bf16)


def query_grads(inner, outer, scale):
    return pl.pallas_call(
        grads_kernel,
        in_specs=[pl.BlockSpec(memory_space=pltpu.VMEM)] * 3,
        out_specs=pl.BlockSpec(memory_space=pltpu.VMEM),
        out_shape=jax.ShapeDtypeStruct((QUERIES, NI * NJ), bf16),
        scratch_shapes=[pltpu.VMEM((NI * NJ, QUERIES), f32)],
        name="query_grads",
    )(inner, outer, scale)


def terms_kernel(core_ref, scaled_ref, store_ref, keep_ref, send_ref):
    me = core_ref[0]
    for r in range(NZ):
        terms = jnp.dot(scaled_ref[...], store_ref[r], preferred_element_type=f32)
        terms = terms.reshape(NW, 2, QUERIES // NF, terms.shape[1])
        first, second = terms[:, 0], terms[:, 1]
        keep_ref[r] = jnp.where(me == 0, first, second)
        send_ref[r] = jnp.where(me == 0, second, first)


def score_terms(core, scaled, store):
    shape = jax.ShapeDtypeStruct((NZ, NW, QUERIES // NF, store.shape[2]), f32)
    return pl.pallas_call(
        terms_kernel,
        in_specs=[pl.BlockSpec(memory_space=pltpu.SMEM)] + [pl.BlockSpec(memory_space=pltpu.VMEM)] * 2,
        out_specs=[pl.BlockSpec(memory_space=pltpu.VMEM)] * 2,
        out_shape=[shape, shape],
        name="score_terms",
    )(core, scaled, store)


def local(acts, out_grads, proj_in, proj_out, assignment, codes, zero_points, scales):
    tokens = acts.shape[0]
    half = tokens // 2
    z = lax.axis_index("z")
    dims = (((0,), (1,)), ((), ()))
    part_inner = lax.dot_general(proj_in, acts, dims, preferred_element_type=f32) * LINK_GAIN
    part_outer = lax.dot_general(proj_out, out_grads, dims, preferred_element_type=f32) * LINK_GAIN
    send_inner = part_inner.astype(f16).reshape(NW, NJ, 2, half).transpose(0, 2, 1, 3)
    send_inner = send_inner.reshape(NF, NJ, half)
    send_outer = part_outer.astype(f16).reshape(NF, NI, tokens)
    inner_terms = exchange(send_inner, FEAT)
    outer_terms = exchange(send_outer, FEAT)
    inner = (jnp.sum(inner_terms.astype(f32), axis=0) * (1.0 / LINK_GAIN)).astype(bf16)
    outer = (jnp.sum(outer_terms.astype(f32), axis=0) * (1.0 / LINK_GAIN)).astype(bf16)

    swap = [((r * NW + w) , (w * NW + r)) for r in range(NZ) for w in range(NW)]
    inner = lax.ppermute(inner, ("z", "yl", "x"), swap)
    inner_all = spread(inner, FEAT, NF)

    outer = outer.reshape(NI, 2, half).transpose(1, 0, 2).reshape(2 * NI, half)
    owners = assignment.reshape(2, half).astype(bf16)
    outer = jnp.concatenate([outer, owners, jnp.zeros((6, half), bf16)], axis=0)
    outer_all = spread(outer, "z", NZ)

    store = store_levels(codes, zero_points).reshape(NZ, NI * NJ, codes.shape[0])
    store_all = exchange(store, "z")

    scale = lax.dynamic_slice_in_dim(scales.reshape(NI, NZ, NJ), z, 1, 1).reshape(1, NI * NJ)
    grads = query_grads(inner_all, outer_all, scale)
    grad_terms = exchange(grads.reshape(4, QUERIES // 4, NI * NJ), "yh")
    share = jnp.sum(grad_terms.astype(f32), axis=0).astype(bf16)
    scaled = spread(share, "yh", 4).reshape(QUERIES, NI * NJ)

    core = lax.axis_index("c").reshape(1).astype(jnp.int32)
    keep, send = score_terms(core, scaled, store_all)
    got = lax.ppermute(send, "c", [(0, 1), (1, 0)])
    terms = (keep + got).astype(bf16).reshape(NZ * NW, QUERIES // NF, codes.shape[0])
    terms = exchange(terms, ("z", "yl", "x"))
    return jnp.sum(terms.astype(f32), axis=0)


def solution(mesh):
    split = Mesh(mesh.devices.reshape(4, 8, 2, 4, 2), AXES)
    in_specs = (
        P(ROWS, FEAT),
        P(ROWS, FEAT),
        P(FEAT, None),
        P(FEAT, None),
        P(ROWS),
        P(ROWS, FEAT),
        P(FEAT),
        P(FEAT),
    )
    out_specs = P(FEAT, ROWS)
    return jax.shard_map(local, mesh=split, in_specs=in_specs, out_specs=out_specs, check_vma=False)
```

time: 299 us -> 176 us (0.59)
  waiting for transfers between devices: 177 us -> 76.9 us
  blocking collectives: 83.4 us -> 16.6 us
  starting transfers between devices: 0.08 us -> 52.7 us
  Pallas kernels: 0 us -> 15.3 us
  between operations: 13.1 us -> 0.15 us
  matrix products: 9.74 us -> 2.71 us
  other arithmetic: 5.6 us -> 2.08 us
    reduce_scatter x2 -> x0, waiting for transfers between devices: 91.3 us -> none  [own_block(): blocks = lax.psum_scatter(blocks, axes[k], scatter_dimension=0, tiled=True)]
    all_gather x1 -> x0, waiting for transfers between devices: 85.2 us -> none  [local(): lax.all_gather(share16, ROWS, axis=0, tiled=True)]
    all_to_all x0 -> x7, waiting for transfers between devices: none -> 75.2 us  [exchange(): return lax.all_to_all(blocks, axes, 0, 0, tiled=True)]
    psum x1 -> x0, blocking collectives: 68.3 us -> none  [local(): summed_inner, summed_outer = lax.psum((part_inner, part_outer), 'feat')]
    all_to_all x0 -> x7, starting transfers between devices: none -> 46.6 us  [exchange(): return lax.all_to_all(blocks, axes, 0, 0, tiled=True)]
    pallas_call x0 -> x3, Pallas kernels: none -> 15.3 us  [the longest x1 8.5 us: query_grads(): pl.pallas_call(grads_kernel, in_specs=[pl.BlockSpec(memory_space=pltpu.VM...]
    another operation x2 -> x0, local copies, waits for them, and re-layouts: 9.55 us -> none  [own_block(): blocks = blocks.reshape(*shape, *blocks.shape[1:])]
    dot_general x4 -> x2, matrix products: 9.74 us -> 2.71 us  [the longest x1 2.22 us: local(): lax.dot_general(proj_out, out_grads, dims, preferred_element_type=f32)]
  transfers between devices with their start and end apart: 3 -> 9, of which waited for: 3 -> 8; matrix products, arithmetic and copies ran while one was open for 0% -> 2% of each run, Pallas kernels for 0% -> 2%
where the time goes in v1:
time: 176 us; the launch traced here: 174 us
  waiting for transfers between devices  76.9 us (44%)
  starting transfers between devices  52.7 us (30%)
  blocking collectives  16.6 us (9%)
  Pallas kernels  15.3 us (9%)
  local copies, waits for them, and re-layouts  7.4 us (4%)
  matrix products  2.71 us (2%)
  other arithmetic  2.08 us (1%)
    all_to_all x7, waiting for transfers between devices, exchange(): return lax.all_to_all(blocks, axes, 0, 0, tiled=True)  75.2 us
    all_to_all x7, starting transfers between devices, exchange(): return lax.all_to_all(blocks, axes, 0, 0, tiled=True)  46.6 us
    all_to_all x1, blocking collectives, exchange(): return lax.all_to_all(blocks, axes, 0, 0, tiled=True)  16.6 us
    pallas_call x1, Pallas kernels, query_grads(): pl.pallas_call(grads_kernel, in_specs=[pl.BlockSpec(memory_space=pltpu.VM...  8.5 us
    ppermute x1, starting transfers between devices, local(): got = lax.ppermute(send, 'c', [(0, 1), (1, 0)])  5.45 us
    pallas_call x1, Pallas kernels, store_levels(): pl.pallas_call(store_kernel, grid=(NI // step,), in_specs=[pl.BlockSpec((...  3.81 us
  transfers between devices with their start and end apart: 9, of which 8 were waited for; matrix products, arithmetic and copies ran while one was open for 2% of the time, Pallas kernels for 2%

profile of v1, /device:TPU:1, one launch (start us, length us, event | category | flops | bytes accessed | tf_op | source)
XLA Modules:
  0.0 173.8 jit_solution(4498906292439415645)
XLA Ops:
  0.0 1.2 copy-done
  1.2 2.2 %fusion.1 = f16[256,1024]{1,0:T(8,128)(2,1)} fusion(bf16[512,256]{1,0:T(8,128)(2,1)} %param.11, bf16[1024,512]{1,0:T(8,128)(2,1)S(1)} %copy-done), kind=kOutput, calls=%fused_computation.3 | convolution fusion | flops 268959744 | bytes 1835008 | tf_op jit(solution)/shard_map/dot_general | solution.py:118
  3.4 10.2 %all-to-all-start.2 = ((f16[16,16,1024]{2,1,0:T(8,128)(2,1)}), f16[16,16,1024]{2,1,0:T(8,128)(2,1)S(1)}, u32[]{:S(2)}, u32[]{:S(2)}) async-start(f16[16,16,1024]{2,1,0:T(8,128)(2,1)} %bitcast.3), calls=%async_computation.2 | async-start | bytes 1048576 | tf_op jit(solution)/shard_map/all_to_all | solution.py:26
  14.6 0.9 copy.10
  15.6 7.8 %all-to-all-done.2 = f16[16,16,1024]{2,1,0:T(8,128)(2,1)S(1)} async-done(((f16[16,16,1024]{2,1,0:T(8,128)(2,1)}), f16[16,16,1024]{2,1,0:T(8,128)(2,1)S(1)}, u32[]{:S(2)}, u32[]{:S(2)}) %all-to-all-start.2) | async-done | bytes 524320 | tf_op jit(solution)/shard_map/all_to_all | solution.py:26
  23.4 4.6 %all-to-all-start = ((f16[16,32,512]{2,1,0:T(8,128)(2,1)}), f16[16,32,512]{2,1,0:T(8,128)(2,1)S(1)}, u32[]{:S(2)}, u32[]{:S(2)}) async-start(f16[16,32,512]{2,1,0:T(8,128)(2,1)} %bitcast.2), calls=%async_computation | async-start | bytes 1048576 | tf_op jit(solution)/shard_map/all_to_all | solution.py:26
  28.4 9.4 %all-to-all-done = f16[16,32,512]{2,1,0:T(8,128)(2,1)S(1)} async-done(((f16[16,32,512]{2,1,0:T(8,128)(2,1)}), f16[16,32,512]{2,1,0:T(8,128)(2,1)S(1)}, u32[]{:S(2)}, u32[]{:S(2)}) %all-to-all-start) | async-done | bytes 524320 | tf_op jit(solution)/shard_map/all_to_all | solution.py:26
  37.8 0.7 broadcast_in_dim.10
  38.5 6.6 %all-to-all-start.3 = ((bf16[8,40,512]{2,1,0:T(8,128)(2,1)}), bf16[8,40,512]{2,1,0:T(8,128)(2,1)S(1)}, u32[]{:S(2)}, u32[]{:S(2)}) async-start(bf16[8,40,512]{2,1,0:T(8,128)(2,1)} %broadcast_in_dim.10), calls=%async_computation.3 | async-start | bytes 655360 | tf_op jit(solution)/shard_map/all_to_all | solution.py:26
  45.2 0.7 collective-permute-start
  45.9 10.5 %all-to-all-done.3.outer_ref = bf16[8,40,512]{2,1,0:T(8,128)(2,1)S(1)} async-done(((bf16[8,40,512]{2,1,0:T(8,128)(2,1)}), bf16[8,40,512]{2,1,0:T(8,128)(2,1)S(1)}, u32[]{:S(2)}, u32[]{:S(2)}) %all-to-all-start.3) | async-done | bytes 327712 | tf_op jit(solution)/shard_map/all_to_all | solution.py:26
  56.4 0.9 broadcast_in_dim.8
  57.3 6.9 %all-to-all-start.1 = ((bf16[16,32,512]{2,1,0:T(8,128)(2,1)}), bf16[16,32,512]{2,1,0:T(8,128)(2,1)S(1)}, u32[]{:S(2)}, u32[]{:S(2)}) async-start(bf16[16,32,512]{2,1,0:T(8,128)(2,1)} %broadcast_in_dim.8), calls=%async_computation.1 | async-start | bytes 1048576 | tf_op jit(solution)/shard_map/all_to_all | solution.py:26
  64.3 0.7 reshape.52.scale_ref
  65.0 8.9 %all-to-all-done.1.inner_ref = bf16[16,32,512]{2,1,0:T(8,128)(2,1)S(1)} async-done(((bf16[16,32,512]{2,1,0:T(8,128)(2,1)}), bf16[16,32,512]{2,1,0:T(8,128)(2,1)S(1)}, u32[]{:S(2)}, u32[]{:S(2)}) %all-to-all-start.1) | async-done | bytes 524320 | tf_op jit(solution)/shard_map/all_to_all | solution.py:26
  73.9 0.8 copy-done.2
  74.7 8.5 %query_grads.1 = bf16[256,512]{1,0:T(8,128)(2,1)} custom-call(bf16[16,32,512]{2,1,0:T(8,128)(2,1)} %copy-done.2, bf16[8,40,512]{2,1,0:T(8,128)(2,1)} %copy-done.3, f32[1,512]{1,0:T(1,128)} %reshape.52.scale_ref), custom_call_target="tpu_custom_call" | custom-call | tf_op jit(solution)/shard_map/query_grads/pallas_call | solution.py:81
  83.2 5.9 %all-to-all-start.4 = ((bf16[4,64,512]{2,1,0:T(8,128)(2,1)}), bf16[4,64,512]{2,1,0:T(8,128)(2,1)S(1)}, u32[]{:S(2)}, u32[]{:S(2)}) async-start(bf16[4,64,512]{2,1,0:T(8,128)(2,1)} %bitcast.18), calls=%async_computation.4 | async-start | bytes 524288 | tf_op jit(solution)/shard_map/all_to_all | solution.py:26
  89.1 3.8 %store_levels.1 = bf16[8,16,32,128]{3,2,1,0:T(8,128)(2,1)} custom-call(s32[128,4096]{1,0:T(8,128)} %codes_ref.1, s32[1,4096]{1,0:T(1,128)} %bitcast.22), custom_call_target="tpu_custom_call" | custom-call | tf_op jit(solution)/shard_map/store_levels/pallas_call | solution.py:43
  92.9 4.3 %all-to-all-done.4 = bf16[4,64,512]{2,1,0:T(8,128)(2,1)S(1)} async-done(((bf16[4,64,512]{2,1,0:T(8,128)(2,1)}), bf16[4,64,512]{2,1,0:T(8,128)(2,1)S(1)}, u32[]{:S(2)}, u32[]{:S(2)}) %all-to-all-start.4) | async-done | bytes 262176 | tf_op jit(solution)/shard_map/all_to_all | solution.py:26
  97.3 4.4 %all-to-all-start.6 = ((bf16[8,512,128]{2,1,0:T(8,128)(2,1)}), bf16[8,512,128]{2,1,0:T(8,128)(2,1)S(1)}, u32[]{:S(2)}, u32[]{:S(2)}) async-start(bf16[8,512,128]{2,1,0:T(8,128)(2,1)} %bitcast.16), calls=%async_computation.6 | async-start | bytes 2097152 | tf_op jit(solution)/shard_map/all_to_all | solution.py:26
  101.7 25.7 %all-to-all-done.6.store_ref = bf16[8,512,128]{2,1,0:T(8,128)(2,1)S(1)} async-done(((bf16[8,512,128]{2,1,0:T(8,128)(2,1)}), bf16[8,512,128]{2,1,0:T(8,128)(2,1)S(1)}, u32[]{:S(2)}, u32[]{:S(2)}) %all-to-all-start.6) | async-done | bytes 1048608 | tf_op jit(solution)/shard_map/all_to_all | solution.py:26
  127.4 0.8 broadcast_in_dim.11
  128.1 7.9 %all-to-all-start.5 = ((bf16[4,64,512]{2,1,0:T(8,128)(2,1)}), bf16[4,64,512]{2,1,0:T(8,128)(2,1)S(1)}, u32[]{:S(2)}, u32[]{:S(2)}) async-start(bf16[4,64,512]{2,1,0:T(8,128)(2,1)} %broadcast_in_dim.11), calls=%async_computation.5 | async-start | bytes 524288 | tf_op jit(solution)/shard_map/all_to_all | solution.py:26
  136.0 8.5 %all-to-all-done.5 = bf16[4,64,512]{2,1,0:T(8,128)(2,1)S(1)} async-done(((bf16[4,64,512]{2,1,0:T(8,128)(2,1)}), bf16[4,64,512]{2,1,0:T(8,128)(2,1)S(1)}, u32[]{:S(2)}, u32[]{:S(2)}) %all-to-all-start.5) | async-done | bytes 262176 | tf_op jit(solution)/shard_map/all_to_all | solution.py:26
  144.5 0.7 copy-done.5
  145.2 3.0 %score_terms.1 = (f32[8,8,16,128]{3,2,1,0:T(8,128)}, f32[8,8,16,128]{3,2,1,0:T(8,128)}) custom-call(s32[1]{0:T(128)} %bitcast.core_ref, bf16[256,512]{1,0:T(8,128)(2,1)} %bitcast.17, bf16[8,512,128]{2,1,0:T(8,128)(2,1)} %copy-done.1), custom_call_target="tpu_custom_call" | custom-call | tf_op jit(solution)/shard_map/score_terms/pallas_call | solution.py:103
  148.2 5.5 %collective-permute-start.1 = (f32[8,8,16,128]{3,2,1,0:T(8,128)}, f32[8,8,16,128]{3,2,1,0:T(8,128)S(1)}, u32[]{:S(2)}, u32[]{:S(2)}) collective-permute-start(f32[8,8,16,128]{3,2,1,0:T(8,128)} %get-tuple-element.8), channel_id=1, source_target_pairs={{0,1},{1,0},{2,3},{3,2},{4,5},{5,4},{6,7},{7,6},{8,9},{9,8},{10,11... | collective-permute-start | bytes 1572872 | tf_op jit(solution)/shard_map/ppermute | solution.py:147
  153.7 1.7 collective-permute-done.1
  155.4 1.1 add_convert_fusion
  156.6 16.6 %all_to_all.40 = bf16[64,16,128]{2,1,0:T(8,128)(2,1)S(1)} all-to-all(bf16[64,16,128]{2,1,0:T(8,128)(2,1)S(1)} %bitcast.19), channel_id=1, replica_groups=mesh['yh'=4,'z'=8,'yl'=2,'x'=4,'c'=2] {'z','yl','x'}, dimensions={0} | all-to-all | bytes 524288 | tf_op jit(solution)/shard_map/all_to_all | solution.py:26
  173.2 0.7 convert_reduce_fusion.2
  (32 shorter events, 1.5 us)
Async XLA Ops:
  0.0 1.2 copy-start
  0.0 13.6 %copy-start.6 = (bf16[512,256]{1,0:T(8,128)(2,1)S(1)}, bf16[512,256]{1,0:T(8,128)(2,1)}, u32[]{:S(2)}) copy-start(bf16[512,256]{1,0:T(8,128)(2,1)} %param.10) | copy-start | bytes 786436
  0.0 13.6 %copy-start.4 = (bf16[1024,512]{1,0:T(8,128)(2,1)S(1)}, bf16[1024,512]{1,0:T(8,128)(2,1)}, u32[]{:S(2)}) copy-start(bf16[1024,512]{1,0:T(8,128)(2,1)} %param.8) | copy-start | bytes 3145732
  3.4 20.0 %all-to-all-start.2 = ((f16[16,16,1024]{2,1,0:T(8,128)(2,1)}), f16[16,16,1024]{2,1,0:T(8,128)(2,1)S(1)}, u32[]{:S(2)}, u32[]{:S(2)}) async-start(f16[16,16,1024]{2,1,0:T(8,128)(2,1)} %bitcast.3), calls=%async_computation.2 | async-start | bytes 1048576 | tf_op jit(solution)/shard_map/all_to_all | solution.py:26
  13.7 14.4 %copy-start.8 = (s32[1024]{0:T(1024)S(1)}, s32[1024]{0:T(1024)}, u32[]{:S(2)}) copy-start(s32[1024]{0:T(1024)} %param.12) | copy-start | bytes 12292
  23.4 14.4 %all-to-all-start = ((f16[16,32,512]{2,1,0:T(8,128)(2,1)}), f16[16,32,512]{2,1,0:T(8,128)(2,1)S(1)}, u32[]{:S(2)}, u32[]{:S(2)}) async-start(f16[16,32,512]{2,1,0:T(8,128)(2,1)} %bitcast.2), calls=%async_computation | async-start | bytes 1048576 | tf_op jit(solution)/shard_map/all_to_all | solution.py:26
  28.1 36.1 %copy-start.7 = (f32[4096]{0:T(1024)S(1)}, f32[4096]{0:T(1024)}, u32[]{:S(2)}) copy-start(f32[4096]{0:T(1024)} %param.15) | copy-start | bytes 49156
  38.5 17.8 %all-to-all-start.3 = ((bf16[8,40,512]{2,1,0:T(8,128)(2,1)}), bf16[8,40,512]{2,1,0:T(8,128)(2,1)S(1)}, u32[]{:S(2)}, u32[]{:S(2)}) async-start(bf16[8,40,512]{2,1,0:T(8,128)(2,1)} %broadcast_in_dim.10), calls=%async_computation.3 | async-start | bytes 655360 | tf_op jit(solution)/shard_map/all_to_all | solution.py:26
  45.2 0.7 collective-permute-start
  56.4 17.5 %copy-start.3 = (bf16[8,40,512]{2,1,0:T(8,128)(2,1)}, bf16[8,40,512]{2,1,0:T(8,128)(2,1)S(1)}, u32[]{:S(2)}) copy-start(bf16[8,40,512]{2,1,0:T(8,128)(2,1)S(1)} %all-to-all-done.3.outer_ref) | copy-start | bytes 983044
  57.3 16.6 %all-to-all-start.1 = ((bf16[16,32,512]{2,1,0:T(8,128)(2,1)}), bf16[16,32,512]{2,1,0:T(8,128)(2,1)S(1)}, u32[]{:S(2)}, u32[]{:S(2)}) async-start(bf16[16,32,512]{2,1,0:T(8,128)(2,1)} %broadcast_in_dim.8), calls=%async_computation.1 | async-start | bytes 1048576 | tf_op jit(solution)/shard_map/all_to_all | solution.py:26
  73.9 0.8 copy-start.2
  83.2 14.1 %all-to-all-start.4 = ((bf16[4,64,512]{2,1,0:T(8,128)(2,1)}), bf16[4,64,512]{2,1,0:T(8,128)(2,1)S(1)}, u32[]{:S(2)}, u32[]{:S(2)}) async-start(bf16[4,64,512]{2,1,0:T(8,128)(2,1)} %bitcast.18), calls=%async_computation.4 | async-start | bytes 524288 | tf_op jit(solution)/shard_map/all_to_all | solution.py:26
  97.3 30.1 %all-to-all-start.6 = ((bf16[8,512,128]{2,1,0:T(8,128)(2,1)}), bf16[8,512,128]{2,1,0:T(8,128)(2,1)S(1)}, u32[]{:S(2)}, u32[]{:S(2)}) async-start(bf16[8,512,128]{2,1,0:T(8,128)(2,1)} %bitcast.16), calls=%async_computation.6 | async-start | bytes 2097152 | tf_op jit(solution)/shard_map/all_to_all | solution.py:26
  127.4 17.2 %copy-start.1 = (bf16[8,512,128]{2,1,0:T(8,128)(2,1)}, bf16[8,512,128]{2,1,0:T(8,128)(2,1)S(1)}, u32[]{:S(2)}) copy-start(bf16[8,512,128]{2,1,0:T(8,128)(2,1)S(1)} %all-to-all-done.6.store_ref) | copy-start | bytes 3145732
  128.1 16.4 %all-to-all-start.5 = ((bf16[4,64,512]{2,1,0:T(8,128)(2,1)}), bf16[4,64,512]{2,1,0:T(8,128)(2,1)S(1)}, u32[]{:S(2)}, u32[]{:S(2)}) async-start(bf16[4,64,512]{2,1,0:T(8,128)(2,1)} %broadcast_in_dim.11), calls=%async_computation.5 | async-start | bytes 524288 | tf_op jit(solution)/shard_map/all_to_all | solution.py:26
  144.5 0.7 copy-start.5
  148.2 7.2 %collective-permute-start.1 = (f32[8,8,16,128]{3,2,1,0:T(8,128)}, f32[8,8,16,128]{3,2,1,0:T(8,128)S(1)}, u32[]{:S(2)}, u32[]{:S(2)}) collective-permute-start(f32[8,8,16,128]{3,2,1,0:T(8,128)} %get-tuple-element.8), channel_id=1, source_target_pairs={{0,1},{1,0},{2,3},{3,2},{4,5},{5,4},{6,7},{7,6},{8,9},{9,8},{10,11... | collective-permute-start | bytes 1572872 | tf_op jit(solution)/shard_map/ppermute | solution.py:147
